TPU v7x, 512 devices: a whole 4x4x16 slice. The times are simulated.
512 devices in a mesh: blk: 16 (over x_lo, y, core), group: 32 (over x_hi, z).
Axes of the slice: x: 4 (x_hi: 2, x_lo: 2; x = x_hi * 2 + x_lo), y: 4, z: 16, core: 2. Of those that a mesh axis runs over, the one named last changes fastest.
Arguments:
- queries: bfloat16 [512, 16, 128], P(('blk', 'group')), may hold values from -2.5 to 2.5
- query_mask: int32 [512, 16], P(('blk', 'group')), may hold values from 0 to 1, as said below
- positive: int32 [512], P(('blk', 'group')), may hold values from 0 to 1023
- page_vectors: bfloat16 [1024, 128, 128], P(('blk', 'group')), may hold values from -2 to 2
- page_mask: int32 [1024, 128], P(('blk', 'group')), may hold values from 0 to 1, as said below
Outputs:
- grad_queries: float32 [512, 16, 128], P(('blk', 'group'))
- grad_pages: float32 [1024, 128, 128], P(('blk', 'group'))
- mean_loss: float32 [], replicated
Inputs may be any that keep to these rules, and one draw needn't show every extreme that they name: `query_mask`: each row holds ones on its first 8 to 16 token slots and zeros after them. `page_mask`: each row holds ones on its first 32 to 128 patch slots and zeros after them.
All inputs are finite; a program needn't handle non-finite values.
Results may differ from a plain program's by a relative error of at most 0.0028.
Values may be sent and summed in bfloat16 or wider, within the bound.
A program may use at most 64 MiB of HBM per device.

v0:
```python
import functools
import math
import jax
import jax.numpy as jnp
from jax import lax
from jax.sharding import Mesh
from jax.sharding import PartitionSpec as P

BLK = ("blk_0", "blk_1", "blk_2")
GROUP = ("group_0", "group_1")
BLK_GROUP = ("blk_0", "blk_1", "blk_2", "group_0", "group_1")
relaxation_scale_factor = 0.5
guarded_floor_entry = -1e30


def side_by_side(arrays, axis, dim, along):
    columns = [a.reshape(*a.shape[:along], -1) for a in arrays]
    both = jnp.concatenate(columns, axis=along)
    result, at, gathered = (lax.all_gather(both, axis, axis=dim, tiled=True), 0, [])
    for a, column in zip(arrays, columns):
        section = result[..., at : at + column.shape[along]]
        gathered.append(section.reshape(*section.shape[:along], *a.shape[along:]))
        at += column.shape[along]
    return tuple(gathered)


def over_axes(x, axes):
    return functools.reduce(lax.pmax, axes, x)


def one_axis_at_a_time(x, axes):
    for axis in axes:
        x = lax.psum(x, axis)
    return x


def from_behind(value, axis, steps):
    count = lax.axis_size(axis)
    pairs = [(source, (source + steps) % count) for source in range(count)]
    return lax.ppermute(value, axis, pairs)


def cut_along(x, dim, size):
    before, after = (x.shape[:dim], x.shape[dim + 1 :])
    return jnp.moveaxis(x.reshape(*before, size, -1, *after), dim, 0)


def sum_at_owner(x, axis, dim):
    size = lax.axis_size(axis)
    pieces = lax.all_to_all(cut_along(x, dim, size), axis, 0, 0, tiled=True)
    return jnp.sum(pieces, axis=0)


def masked_logits(row_block, lone_document, live_image_embeddings):
    similarity_matrix = lax.dot_general(
        row_block, lone_document, (((1,), (1,)), ((), ())), preferred_element_type=jnp.float32
    )
    return jnp.where(
        live_image_embeddings[None, :] > 0,
        similarity_matrix / relaxation_scale_factor,
        guarded_floor_entry,
    )


def on_device(queries, query_mask, positive, page_vectors, page_mask):
    tokens = queries.shape[1]
    features = queries.shape[2]
    local_pages = page_vectors.shape[0]
    blocks = lax.axis_size(BLK)
    members = lax.axis_size(GROUP)
    bundle_size = queries.shape[0] * members
    total_queries = bundle_size * blocks
    natural_logarithm_lengths = jnp.log(jnp.sum(page_mask.astype(jnp.float32), axis=1))
    bundle_vectors, bundle_masks, bundle_targets = (
        lax.all_gather(queries, GROUP, axis=0, tiled=True),
        *side_by_side((query_mask, positive), GROUP, 0, 1),
    )

    def forward_piece(folded, shard_in, root_row):
        scores, lse_rows, live_all, owners, kept = folded
        vectors, token_masks, targets = shard_in
        amount = vectors.shape[0]
        stride = math.gcd(amount, max(1, 512 // tokens))

        def run_block(number, current):
            scores, lse_rows = current
            offset = number * stride
            slab_rows = lax.dynamic_slice_in_dim(vectors, offset, stride, 0).reshape(
                stride * tokens, features
            )
            alive = lax.dynamic_slice_in_dim(token_masks, offset, stride, 0).astype(jnp.float32)
            found_sums = []
            for index_page in range(local_pages):
                masked = masked_logits(slab_rows, page_vectors[index_page], page_mask[index_page])
                highest = jnp.max(masked, axis=1, keepdims=True)
                found_sums.append(
                    highest[:, 0] + jnp.log(jnp.sum(jnp.exp(masked - highest), axis=1))
                )
            logsumexp_results = jnp.stack(found_sums, axis=1).reshape(stride, tokens, local_pages)
            softened_supremum = relaxation_scale_factor * (
                logsumexp_results - natural_logarithm_lengths
            )
            page_score = jnp.sum(alive[:, :, None] * softened_supremum, axis=1)
            scores = lax.dynamic_update_slice_in_dim(scores, page_score, offset, 0)
            lse_rows = lax.dynamic_update_slice_in_dim(lse_rows, logsumexp_results, offset, 0)
            return (scores, lse_rows)

        scores, lse_rows = lax.fori_loop(0, amount // stride, run_block, (scores, lse_rows))
        live_all = lax.dynamic_update_slice_in_dim(live_all, token_masks, root_row, 0)
        owners = lax.dynamic_update_slice_in_dim(owners, targets, root_row, 0)
        kept = vectors
        return (scores, lse_rows, live_all, owners, kept)

    starting = (
        jnp.zeros((total_queries, local_pages), jnp.float32),
        jnp.zeros((total_queries, tokens, local_pages), jnp.float32),
        jnp.zeros((total_queries, tokens), jnp.int32),
        jnp.zeros((total_queries,), jnp.int32),
        jnp.zeros((total_queries, tokens, features), jnp.bfloat16),
    )
    scores, lse_rows, live_all, owners, kept = forward_piece(
        starting,
        (
            lax.all_gather(bundle_vectors, BLK, axis=0, tiled=True),
            lax.all_gather(bundle_masks, BLK, axis=0, tiled=True),
            lax.all_gather(bundle_targets, BLK, axis=0, tiled=True),
        ),
        jnp.int32(0),
    )
    position = lax.axis_index(BLK_GROUP)
    page_ids = position * local_pages + jnp.arange(local_pages, dtype=jnp.int32)
    chosen = owners[:, None] == page_ids[None, :]
    picked_local = jnp.sum(jnp.where(chosen, scores, 0.0))
    local_top = jnp.max(scores, axis=1)
    highest = over_axes(local_top, BLK_GROUP)
    local_total = jnp.sum(jnp.exp(scores - highest[:, None]), axis=1)
    totals, picked = (
        one_axis_at_a_time(local_total, BLK_GROUP),
        one_axis_at_a_time(picked_local, BLK_GROUP),
    )
    page_lse = highest + jnp.log(totals)
    mean_loss = (jnp.sum(page_lse) - picked) / total_queries
    coefficient = jnp.exp(scores - page_lse[:, None]) - chosen.astype(jnp.float32)
    factor_scale = coefficient[:, None, :] * live_all.astype(jnp.float32)[:, :, None]

    def slice_rows(root_row, amount):
        sums = lax.dynamic_slice_in_dim(lse_rows, root_row, amount, 0).reshape(
            amount * tokens, local_pages
        )
        scales = lax.dynamic_slice_in_dim(factor_scale, root_row, amount, 0).reshape(
            amount * tokens, local_pages
        )
        return (sums, scales)

    def gradient_terms(row_block, logsumexp_results, scales, page_grads):
        partial_value = jnp.zeros(row_block.shape, jnp.float32)
        for number in range(local_pages):
            masked = masked_logits(row_block, page_vectors[number], page_mask[number])
            weights = jnp.exp(masked - logsumexp_results[:, number : number + 1])
            factor = (scales[:, number : number + 1] * weights).astype(jnp.bfloat16)
            partial_value = partial_value + jnp.dot(
                factor, page_vectors[number], preferred_element_type=jnp.float32
            )
            update = lax.dot_general(
                factor, row_block, (((0,), (0,)), ((), ())), preferred_element_type=jnp.float32
            )
            page_grads = page_grads.at[number].add(update)
        return (partial_value, page_grads)

    home = lax.axis_index(BLK)
    page_grads = jnp.zeros(page_vectors.shape, jnp.float32)

    def visit_one(moving, collected, page_grads, lap_index):
        root_row = (home - lap_index) % blocks * bundle_size
        sums, scales = slice_rows(root_row, bundle_size)
        partial_value, page_grads = gradient_terms(
            moving.reshape(bundle_size * tokens, features), sums, scales, page_grads
        )
        return (collected + partial_value.reshape(bundle_size, tokens, features), page_grads)

    def pass_one(collected):
        return from_behind(collected, BLK, 1)

    def turn_one(lap_index, current):
        moving, collected, page_grads = current
        collected, page_grads = visit_one(moving, collected, page_grads, lap_index)
        moving = from_behind(moving, BLK, 1)
        return (moving, pass_one(collected), page_grads)

    empty_whole = jnp.zeros((bundle_size, tokens, features), jnp.float32)
    moving, collected, page_grads = lax.fori_loop(
        0, blocks - 1, turn_one, (bundle_vectors, empty_whole, page_grads)
    )
    collected, page_grads = visit_one(moving, collected, page_grads, blocks - 1)
    collected = pass_one(collected)
    grad_queries = sum_at_owner(collected, GROUP, 0)
    return (grad_queries, page_grads, mean_loss)


def solution(mesh):
    split = Mesh(
        mesh.devices.reshape(2, 4, 2, 2, 16), ("blk_0", "blk_1", "blk_2", "group_0", "group_1")
    )
    return jax.shard_map(
        on_device,
        mesh=split,
        in_specs=(
            P(BLK_GROUP, None, None),
            P(BLK_GROUP, None),
            P(BLK_GROUP),
            P(BLK_GROUP, None, None),
            P(BLK_GROUP, None),
        ),
        out_specs=(P(BLK_GROUP, None, None), P(BLK_GROUP, None, None), P()),
        check_vma=False,
    )
```

profile of v0, /device:TPU:2, one launch (start us, length us, event | category | flops | bytes accessed | tf_op | source)
XLA Modules:
  0.0 667.9 jit_solution(16827437556974625158)
XLA Ops:
  7.2 87.3 %all_gather.15 = bf16[32,16,128]{2,1,0:T(8,128)(2,1)} all-gather(bf16[1,16,128]{2,1,0:T(8,128)(2,1)} %param.17), channel_id=1, replica_groups=mesh['blk_0'=2,'blk_1'=4,'blk_2'=2,'group_0'=2,'group_1'=16] {'group_0',..., dimensions={0}, use_global_device_ids=true | all-gather | bytes 135168 | tf_op jit(solution)/shard_map/all_gather | solution.py:75
  95.9 70.5 %all-gather.1 = s32[32,1,17]{2,1,0:T(1,128)S(1)} all-gather(s32[1,1,17]{2,1,0:T(1,128)S(1)} %add_bitcast_fusion), channel_id=1, replica_groups=mesh['blk_0'=2,'blk_1'=4,'blk_2'=2,'group_0'=2,'group_1'=16] {'group_0',..., dimensions={0}, use_global_device_ids=true | all-gather | bytes 2244 | tf_op jit(solution)/shard_map/all_gather | solution.py:19
  166.4 20.1 %all-gather.2 = s32[16,32,16]{1,2,0:T(8,128)S(1)} all-gather(s32[1,32,16]{1,2,0:T(8,128)S(1)} %copy.11), channel_id=1, replica_groups=mesh['blk_0'=2,'blk_1'=4,'blk_2'=2,'group_0'=2,'group_1'=16] {'blk_0','b..., dimensions={0}, use_global_device_ids=true | all-gather | bytes 34816 | tf_op jit(solution)/shard_map/all_gather | solution.py:125
  190.0 8.0 %all-reduce = s32[512]{0:T(512)S(1)} all-reduce(s32[512]{0:T(512)S(1)} %dynamic-update-slice.26), channel_id=2, replica_groups=mesh['blk_0'=2,'blk_1'=4,'blk_2'=2,'group_0'=2,'group_1'=16] {'blk_0','b..., use_global_device_ids=true, to_apply=%add | all-reduce | flops 512 | bytes 4096
  198.9 72.4 %while.38 = (s32[]{:T(128)}, f32[512,2]{0,1:T(2,128)S(1)}, f32[512,16,2]{1,0,2:T(8,128)S(1)}, s32[2,128]{1,0:T(2,128)}, bf16[512,16,128]{2,1,0:T(8,128)(2,1)}, /...) while((s32[]{:T(128)}, f32[512,2]{0,1:T(2,128)S(1)}, ...), condition=%wide.region_7.8_spmd, body=%wide.region_1.7_spmd.sunk | while | flops 34213060 | bytes 1820339 | solution.py:108
  271.3 4.9 pmax.35
  276.2 11.6 %pmax.36 = f32[512]{0:T(512)S(1)} all-reduce(f32[512]{0:T(512)S(1)} %pmax.35), channel_id=1, replica_groups=mesh['blk_0'=2,'blk_1'=4,'blk_2'=2,'group_0'=2,'group_1'=16] {'blk_1'}, use_global_device_ids=true, to_apply=%region_10.11 | all-reduce | flops 512 | bytes 4096 | tf_op jit(solution)/shard_map/pmax | solution.py:28
  287.8 2.5 pmax.37
  290.2 6.4 pmax.38
  296.7 29.0 %pmax.39 = f32[512]{0:T(512)S(1)} all-reduce(f32[512]{0:T(512)S(1)} %pmax.38), channel_id=1, replica_groups=mesh['blk_0'=2,'blk_1'=4,'blk_2'=2,'group_0'=2,'group_1'=16] {'group_1'}, use_global_device_ids=true, to_apply=%region_13.14 | all-reduce | flops 512 | bytes 4096 | tf_op jit(solution)/shard_map/pmax | solution.py:28
  326.4 5.5 all-reduce.5
  331.9 8.3 %all-reduce.2 = (f32[512]{0:T(512)S(1)}, f32[]{:T(128)}) all-reduce(f32[512]{0:T(512)S(1)} %get-tuple-element.502, f32[]{:T(128)} %get-tuple-element.503), channel_id=1, replica_groups=mesh['blk_0'=2,'blk_1'=4,'blk_2'=2,'group_0'=2,'group_1'=16] {'blk_1'}, use_global_device_ids=true, to_apply=%region_16.17 | all-reduce | flops 513 | bytes 4104 | tf_op jit(solution)/shard_map/psum | solution.py:33
  340.3 3.1 all-reduce.4
  343.3 7.0 %all-reduce.3 = (f32[512]{0:T(512)S(1)}, f32[]{:T(128)}) all-reduce(f32[512]{0:T(512)S(1)} %get-tuple-element.500, f32[]{:T(128)} %get-tuple-element.501), channel_id=1, replica_groups=mesh['blk_0'=2,'blk_1'=4,'blk_2'=2,'group_0'=2,'group_1'=16] {'group_0'}, use_global_device_ids=true, to_apply=%region_18.19 | all-reduce | flops 513 | bytes 4104 | tf_op jit(solution)/shard_map/psum | solution.py:33
  350.4 27.6 %all-reduce.1 = (f32[512]{0:T(512)S(1)}, f32[]{:T(128)}) all-reduce(f32[512]{0:T(512)S(1)} %get-tuple-element.498, f32[]{:T(128)} %get-tuple-element.499), channel_id=1, replica_groups=mesh['blk_0'=2,'blk_1'=4,'blk_2'=2,'group_0'=2,'group_1'=16] {'group_1'}, use_global_device_ids=true, to_apply=%region_19.20 | all-reduce | flops 513 | bytes 4104 | tf_op jit(solution)/shard_map/psum | solution.py:33
  379.3 240.3 %while.39 = (s32[]{:T(128)}, bf16[32,16,128]{2,1,0:T(8,128)(2,1)S(1)}, f32[32,16,128]{2,1,0:T(8,128)S(1)}, f32[2,128,128]{2,1,0:T(8,128)S(1)}, s32[]{:T(128)}, /...) while((s32[]{:T(128)}, ...), condition=%wide.region_21.22_spmd, body=%wide.region_20.21_spmd.sunk | while | flops 101482768 | bytes 5433252 | solution.py:191
  379.3 1.9 collective-permute-start
  385.4 4.0 collective-permute-start.1
  389.9 5.3 collective-permute-done.1
  395.2 2.1 collective-permute-start
  401.4 1.9 collective-permute-start.1
  403.8 7.4 %collective-permute-done.1 = f32[32,16,128]{2,1,0:T(8,128)S(1)} collective-permute-done((f32[32,16,128]{2,1,0:T(8,128)S(1)}, f32[32,16,128]{2,1,0:T(8,128)S(1)}, u32[]{:S(2)}, u32[]{:S(2)}) %collective-permute-start.1) | collective-permute-done | bytes 262176 | tf_op jit(solution)/shard_map/while/body/eval_jaxpr/ppermute | solution.py:40
  411.2 2.1 collective-permute-start
  417.4 1.9 collective-permute-start.1
  419.8 7.4 %collective-permute-done.1 = f32[32,16,128]{2,1,0:T(8,128)S(1)} collective-permute-done((f32[32,16,128]{2,1,0:T(8,128)S(1)}, f32[32,16,128]{2,1,0:T(8,128)S(1)}, u32[]{:S(2)}, u32[]{:S(2)}) %collective-permute-start.1) | collective-permute-done | bytes 262176 | tf_op jit(solution)/shard_map/while/body/eval_jaxpr/ppermute | solution.py:40
  427.2 2.1 collective-permute-start
  433.5 1.9 collective-permute-start.1
  435.9 7.4 %collective-permute-done.1 = f32[32,16,128]{2,1,0:T(8,128)S(1)} collective-permute-done((f32[32,16,128]{2,1,0:T(8,128)S(1)}, f32[32,16,128]{2,1,0:T(8,128)S(1)}, u32[]{:S(2)}, u32[]{:S(2)}) %collective-permute-start.1) | collective-permute-done | bytes 262176 | tf_op jit(solution)/shard_map/while/body/eval_jaxpr/ppermute | solution.py:40
  443.3 2.1 collective-permute-start
  449.5 1.9 collective-permute-start.1
  451.9 7.4 %collective-permute-done.1 = f32[32,16,128]{2,1,0:T(8,128)S(1)} collective-permute-done((f32[32,16,128]{2,1,0:T(8,128)S(1)}, f32[32,16,128]{2,1,0:T(8,128)S(1)}, u32[]{:S(2)}, u32[]{:S(2)}) %collective-permute-start.1) | collective-permute-done | bytes 262176 | tf_op jit(solution)/shard_map/while/body/eval_jaxpr/ppermute | solution.py:40
  459.3 2.1 collective-permute-start
  465.5 1.9 collective-permute-start.1
  467.9 7.4 %collective-permute-done.1 = f32[32,16,128]{2,1,0:T(8,128)S(1)} collective-permute-done((f32[32,16,128]{2,1,0:T(8,128)S(1)}, f32[32,16,128]{2,1,0:T(8,128)S(1)}, u32[]{:S(2)}, u32[]{:S(2)}) %collective-permute-start.1) | collective-permute-done | bytes 262176 | tf_op jit(solution)/shard_map/while/body/eval_jaxpr/ppermute | solution.py:40
  475.3 2.1 collective-permute-start
  481.5 1.9 collective-permute-start.1
  483.9 7.4 %collective-permute-done.1 = f32[32,16,128]{2,1,0:T(8,128)S(1)} collective-permute-done((f32[32,16,128]{2,1,0:T(8,128)S(1)}, f32[32,16,128]{2,1,0:T(8,128)S(1)}, u32[]{:S(2)}, u32[]{:S(2)}) %collective-permute-start.1) | collective-permute-done | bytes 262176 | tf_op jit(solution)/shard_map/while/body/eval_jaxpr/ppermute | solution.py:40
  491.3 2.1 collective-permute-start
  497.6 1.9 collective-permute-start.1
  500.0 7.4 %collective-permute-done.1 = f32[32,16,128]{2,1,0:T(8,128)S(1)} collective-permute-done((f32[32,16,128]{2,1,0:T(8,128)S(1)}, f32[32,16,128]{2,1,0:T(8,128)S(1)}, u32[]{:S(2)}, u32[]{:S(2)}) %collective-permute-start.1) | collective-permute-done | bytes 262176 | tf_op jit(solution)/shard_map/while/body/eval_jaxpr/ppermute | solution.py:40
  507.4 2.1 collective-permute-start
  513.6 1.9 collective-permute-start.1
  516.0 7.4 %collective-permute-done.1 = f32[32,16,128]{2,1,0:T(8,128)S(1)} collective-permute-done((f32[32,16,128]{2,1,0:T(8,128)S(1)}, f32[32,16,128]{2,1,0:T(8,128)S(1)}, u32[]{:S(2)}, u32[]{:S(2)}) %collective-permute-start.1) | collective-permute-done | bytes 262176 | tf_op jit(solution)/shard_map/while/body/eval_jaxpr/ppermute | solution.py:40
  523.4 2.1 collective-permute-start
  529.6 1.9 collective-permute-start.1
  532.0 7.4 %collective-permute-done.1 = f32[32,16,128]{2,1,0:T(8,128)S(1)} collective-permute-done((f32[32,16,128]{2,1,0:T(8,128)S(1)}, f32[32,16,128]{2,1,0:T(8,128)S(1)}, u32[]{:S(2)}, u32[]{:S(2)}) %collective-permute-start.1) | collective-permute-done | bytes 262176 | tf_op jit(solution)/shard_map/while/body/eval_jaxpr/ppermute | solution.py:40
  539.4 2.1 collective-permute-start
  545.6 1.9 collective-permute-start.1
  548.0 7.4 %collective-permute-done.1 = f32[32,16,128]{2,1,0:T(8,128)S(1)} collective-permute-done((f32[32,16,128]{2,1,0:T(8,128)S(1)}, f32[32,16,128]{2,1,0:T(8,128)S(1)}, u32[]{:S(2)}, u32[]{:S(2)}) %collective-permute-start.1) | collective-permute-done | bytes 262176 | tf_op jit(solution)/shard_map/while/body/eval_jaxpr/ppermute | solution.py:40
  555.4 2.1 collective-permute-start
  561.7 1.9 collective-permute-start.1
  564.1 7.4 %collective-permute-done.1 = f32[32,16,128]{2,1,0:T(8,128)S(1)} collective-permute-done((f32[32,16,128]{2,1,0:T(8,128)S(1)}, f32[32,16,128]{2,1,0:T(8,128)S(1)}, u32[]{:S(2)}, u32[]{:S(2)}) %collective-permute-start.1) | collective-permute-done | bytes 262176 | tf_op jit(solution)/shard_map/while/body/eval_jaxpr/ppermute | solution.py:40
  571.5 2.1 collective-permute-start
  580.1 7.4 %collective-permute-done.1 = f32[32,16,128]{2,1,0:T(8,128)S(1)} collective-permute-done((f32[32,16,128]{2,1,0:T(8,128)S(1)}, f32[32,16,128]{2,1,0:T(8,128)S(1)}, u32[]{:S(2)}, u32[]{:S(2)}) %collective-permute-start.1) | collective-permute-done | bytes 262176 | tf_op jit(solution)/shard_map/while/body/eval_jaxpr/ppermute | solution.py:40
  587.5 2.1 collective-permute-start
  593.7 1.9 collective-permute-start.1
  596.1 7.4 %collective-permute-done.1 = f32[32,16,128]{2,1,0:T(8,128)S(1)} collective-permute-done((f32[32,16,128]{2,1,0:T(8,128)S(1)}, f32[32,16,128]{2,1,0:T(8,128)S(1)}, u32[]{:S(2)}, u32[]{:S(2)}) %collective-permute-start.1) | collective-permute-done | bytes 262176 | tf_op jit(solution)/shard_map/while/body/eval_jaxpr/ppermute | solution.py:40
  603.5 2.1 collective-permute-start
  609.7 1.9 collective-permute-start.1
  612.1 7.4 %collective-permute-done.1 = f32[32,16,128]{2,1,0:T(8,128)S(1)} collective-permute-done((f32[32,16,128]{2,1,0:T(8,128)S(1)}, f32[32,16,128]{2,1,0:T(8,128)S(1)}, u32[]{:S(2)}, u32[]{:S(2)}) %collective-permute-start.1) | collective-permute-done | bytes 262176 | tf_op jit(solution)/shard_map/while/body/eval_jaxpr/ppermute | solution.py:40
  623.4 1.9 collective-permute-start.2
  625.4 8.0 %collective-permute-done.2 = f32[32,16,128]{2,1,0:T(8,128)} collective-permute-done((f32[32,16,128]{2,1,0:T(8,128)S(1)}, f32[32,16,128]{2,1,0:T(8,128)}, u32[]{:S(2)}, u32[]{:S(2)}) %collective-permute-start.2) | collective-permute-done | bytes 262176 | tf_op jit(solution)/shard_map/ppermute | solution.py:40
  633.3 6.3 all-to-all-start
  641.4 17.8 %all-to-all-done = f32[32,1,16,128]{3,2,1,0:T(8,128)S(1)} async-done(((f32[32,1,16,128]{3,2,1,0:T(8,128)}), f32[32,1,16,128]{3,2,1,0:T(8,128)S(1)}, u32[]{:S(2)}, u32[]{:S(2)}) %all-to-all-start) | async-done | bytes 262176 | tf_op jit(solution)/shard_map/all_to_all | solution.py:50
  (573 shorter events, 153.2 us)
Async XLA Ops:
  7.2 191.7 %all-gather.5.cloned.1.call-start = ((), (), s32[]{:S(2)}) async-start(), calls=%async_computation.1 | async-start | bytes 2228224 | tf_op jit(solution)/shard_map/all_gather | solution.py:124
  198.9 180.4 %copy-start = (bf16[32,16,128]{2,1,0:T(8,128)(2,1)S(1)}, bf16[32,16,128]{2,1,0:T(8,128)(2,1)}, u32[]{:S(2)}) copy-start(bf16[32,16,128]{2,1,0:T(8,128)(2,1)} %all_gather.15) | copy-start | bytes 393220
  379.3 5.9 copy-start.1
  379.3 10.6 %collective-permute-start = (bf16[32,16,128]{2,1,0:T(8,128)(2,1)S(1)}, bf16[32,16,128]{2,1,0:T(8,128)(2,1)S(1)}, u32[]{:S(2)}, u32[]{:S(2)}) collective-permute-start(bf16[32,16,128]{2,1,0:T(8,128)(2,1)S(1)} %copy.38), channel_id=1, source_target_pairs={{0,32},{32,64},{64,96},{96,128},{128,160},{160,192},{192,224},{224... | collective-permute-start | bytes 393224 | tf_op jit(solution)/shard_map/while/body/eval_jaxpr/ppermute | solution.py:40
  385.4 9.8 %collective-permute-start.1 = (f32[32,16,128]{2,1,0:T(8,128)S(1)}, f32[32,16,128]{2,1,0:T(8,128)S(1)}, u32[]{:S(2)}, u32[]{:S(2)}) collective-permute-start(f32[32,16,128]{2,1,0:T(8,128)S(1)} %add.300), channel_id=1, source_target_pairs={{0,32},{32,64},{64,96},{96,128},{128,160},{160,192},{192,224},{224... | collective-permute-start | bytes 786440 | tf_op jit(solution)/shard_map/while/body/eval_jaxpr/ppermute | solution.py:40
  395.2 6.0 copy-start.1
  395.2 8.6 %collective-permute-start = (bf16[32,16,128]{2,1,0:T(8,128)(2,1)S(1)}, bf16[32,16,128]{2,1,0:T(8,128)(2,1)S(1)}, u32[]{:S(2)}, u32[]{:S(2)}) collective-permute-start(bf16[32,16,128]{2,1,0:T(8,128)(2,1)S(1)} %copy.38), channel_id=1, source_target_pairs={{0,32},{32,64},{64,96},{96,128},{128,160},{160,192},{192,224},{224... | collective-permute-start | bytes 393224 | tf_op jit(solution)/shard_map/while/body/eval_jaxpr/ppermute | solution.py:40
  401.4 9.8 %collective-permute-start.1 = (f32[32,16,128]{2,1,0:T(8,128)S(1)}, f32[32,16,128]{2,1,0:T(8,128)S(1)}, u32[]{:S(2)}, u32[]{:S(2)}) collective-permute-start(f32[32,16,128]{2,1,0:T(8,128)S(1)} %add.300), channel_id=1, source_target_pairs={{0,32},{32,64},{64,96},{96,128},{128,160},{160,192},{192,224},{224... | collective-permute-start | bytes 786440 | tf_op jit(solution)/shard_map/while/body/eval_jaxpr/ppermute | solution.py:40
  411.2 6.0 copy-start.1
  411.2 8.6 %collective-permute-start = (bf16[32,16,128]{2,1,0:T(8,128)(2,1)S(1)}, bf16[32,16,128]{2,1,0:T(8,128)(2,1)S(1)}, u32[]{:S(2)}, u32[]{:S(2)}) collective-permute-start(bf16[32,16,128]{2,1,0:T(8,128)(2,1)S(1)} %copy.38), channel_id=1, source_target_pairs={{0,32},{32,64},{64,96},{96,128},{128,160},{160,192},{192,224},{224... | collective-permute-start | bytes 393224 | tf_op jit(solution)/shard_map/while/body/eval_jaxpr/ppermute | solution.py:40
  417.4 9.8 %collective-permute-start.1 = (f32[32,16,128]{2,1,0:T(8,128)S(1)}, f32[32,16,128]{2,1,0:T(8,128)S(1)}, u32[]{:S(2)}, u32[]{:S(2)}) collective-permute-start(f32[32,16,128]{2,1,0:T(8,128)S(1)} %add.300), channel_id=1, source_target_pairs={{0,32},{32,64},{64,96},{96,128},{128,160},{160,192},{192,224},{224... | collective-permute-start | bytes 786440 | tf_op jit(solution)/shard_map/while/body/eval_jaxpr/ppermute | solution.py:40
  427.2 6.0 copy-start.1
  427.2 8.6 %collective-permute-start = (bf16[32,16,128]{2,1,0:T(8,128)(2,1)S(1)}, bf16[32,16,128]{2,1,0:T(8,128)(2,1)S(1)}, u32[]{:S(2)}, u32[]{:S(2)}) collective-permute-start(bf16[32,16,128]{2,1,0:T(8,128)(2,1)S(1)} %copy.38), channel_id=1, source_target_pairs={{0,32},{32,64},{64,96},{96,128},{128,160},{160,192},{192,224},{224... | collective-permute-start | bytes 393224 | tf_op jit(solution)/shard_map/while/body/eval_jaxpr/ppermute | solution.py:40
  433.5 9.8 %collective-permute-start.1 = (f32[32,16,128]{2,1,0:T(8,128)S(1)}, f32[32,16,128]{2,1,0:T(8,128)S(1)}, u32[]{:S(2)}, u32[]{:S(2)}) collective-permute-start(f32[32,16,128]{2,1,0:T(8,128)S(1)} %add.300), channel_id=1, source_target_pairs={{0,32},{32,64},{64,96},{96,128},{128,160},{160,192},{192,224},{224... | collective-permute-start | bytes 786440 | tf_op jit(solution)/shard_map/while/body/eval_jaxpr/ppermute | solution.py:40
  443.3 6.0 copy-start.1
  443.3 8.6 %collective-permute-start = (bf16[32,16,128]{2,1,0:T(8,128)(2,1)S(1)}, bf16[32,16,128]{2,1,0:T(8,128)(2,1)S(1)}, u32[]{:S(2)}, u32[]{:S(2)}) collective-permute-start(bf16[32,16,128]{2,1,0:T(8,128)(2,1)S(1)} %copy.38), channel_id=1, source_target_pairs={{0,32},{32,64},{64,96},{96,128},{128,160},{160,192},{192,224},{224... | collective-permute-start | bytes 393224 | tf_op jit(solution)/shard_map/while/body/eval_jaxpr/ppermute | solution.py:40
  449.5 9.8 %collective-permute-start.1 = (f32[32,16,128]{2,1,0:T(8,128)S(1)}, f32[32,16,128]{2,1,0:T(8,128)S(1)}, u32[]{:S(2)}, u32[]{:S(2)}) collective-permute-start(f32[32,16,128]{2,1,0:T(8,128)S(1)} %add.300), channel_id=1, source_target_pairs={{0,32},{32,64},{64,96},{96,128},{128,160},{160,192},{192,224},{224... | collective-permute-start | bytes 786440 | tf_op jit(solution)/shard_map/while/body/eval_jaxpr/ppermute | solution.py:40
  459.3 6.0 copy-start.1
  459.3 8.6 %collective-permute-start = (bf16[32,16,128]{2,1,0:T(8,128)(2,1)S(1)}, bf16[32,16,128]{2,1,0:T(8,128)(2,1)S(1)}, u32[]{:S(2)}, u32[]{:S(2)}) collective-permute-start(bf16[32,16,128]{2,1,0:T(8,128)(2,1)S(1)} %copy.38), channel_id=1, source_target_pairs={{0,32},{32,64},{64,96},{96,128},{128,160},{160,192},{192,224},{224... | collective-permute-start | bytes 393224 | tf_op jit(solution)/shard_map/while/body/eval_jaxpr/ppermute | solution.py:40
  465.5 9.8 %collective-permute-start.1 = (f32[32,16,128]{2,1,0:T(8,128)S(1)}, f32[32,16,128]{2,1,0:T(8,128)S(1)}, u32[]{:S(2)}, u32[]{:S(2)}) collective-permute-start(f32[32,16,128]{2,1,0:T(8,128)S(1)} %add.300), channel_id=1, source_target_pairs={{0,32},{32,64},{64,96},{96,128},{128,160},{160,192},{192,224},{224... | collective-permute-start | bytes 786440 | tf_op jit(solution)/shard_map/while/body/eval_jaxpr/ppermute | solution.py:40
  475.3 6.0 copy-start.1
  475.3 8.6 %collective-permute-start = (bf16[32,16,128]{2,1,0:T(8,128)(2,1)S(1)}, bf16[32,16,128]{2,1,0:T(8,128)(2,1)S(1)}, u32[]{:S(2)}, u32[]{:S(2)}) collective-permute-start(bf16[32,16,128]{2,1,0:T(8,128)(2,1)S(1)} %copy.38), channel_id=1, source_target_pairs={{0,32},{32,64},{64,96},{96,128},{128,160},{160,192},{192,224},{224... | collective-permute-start | bytes 393224 | tf_op jit(solution)/shard_map/while/body/eval_jaxpr/ppermute | solution.py:40
  481.5 9.8 %collective-permute-start.1 = (f32[32,16,128]{2,1,0:T(8,128)S(1)}, f32[32,16,128]{2,1,0:T(8,128)S(1)}, u32[]{:S(2)}, u32[]{:S(2)}) collective-permute-start(f32[32,16,128]{2,1,0:T(8,128)S(1)} %add.300), channel_id=1, source_target_pairs={{0,32},{32,64},{64,96},{96,128},{128,160},{160,192},{192,224},{224... | collective-permute-start | bytes 786440 | tf_op jit(solution)/shard_map/while/body/eval_jaxpr/ppermute | solution.py:40
  491.3 6.0 copy-start.1
  491.3 8.6 %collective-permute-start = (bf16[32,16,128]{2,1,0:T(8,128)(2,1)S(1)}, bf16[32,16,128]{2,1,0:T(8,128)(2,1)S(1)}, u32[]{:S(2)}, u32[]{:S(2)}) collective-permute-start(bf16[32,16,128]{2,1,0:T(8,128)(2,1)S(1)} %copy.38), channel_id=1, source_target_pairs={{0,32},{32,64},{64,96},{96,128},{128,160},{160,192},{192,224},{224... | collective-permute-start | bytes 393224 | tf_op jit(solution)/shard_map/while/body/eval_jaxpr/ppermute | solution.py:40
  497.6 9.8 %collective-permute-start.1 = (f32[32,16,128]{2,1,0:T(8,128)S(1)}, f32[32,16,128]{2,1,0:T(8,128)S(1)}, u32[]{:S(2)}, u32[]{:S(2)}) collective-permute-start(f32[32,16,128]{2,1,0:T(8,128)S(1)} %add.300), channel_id=1, source_target_pairs={{0,32},{32,64},{64,96},{96,128},{128,160},{160,192},{192,224},{224... | collective-permute-start | bytes 786440 | tf_op jit(solution)/shard_map/while/body/eval_jaxpr/ppermute | solution.py:40
  507.4 6.0 copy-start.1
  507.4 8.6 %collective-permute-start = (bf16[32,16,128]{2,1,0:T(8,128)(2,1)S(1)}, bf16[32,16,128]{2,1,0:T(8,128)(2,1)S(1)}, u32[]{:S(2)}, u32[]{:S(2)}) collective-permute-start(bf16[32,16,128]{2,1,0:T(8,128)(2,1)S(1)} %copy.38), channel_id=1, source_target_pairs={{0,32},{32,64},{64,96},{96,128},{128,160},{160,192},{192,224},{224... | collective-permute-start | bytes 393224 | tf_op jit(solution)/shard_map/while/body/eval_jaxpr/ppermute | solution.py:40
  513.6 9.8 %collective-permute-start.1 = (f32[32,16,128]{2,1,0:T(8,128)S(1)}, f32[32,16,128]{2,1,0:T(8,128)S(1)}, u32[]{:S(2)}, u32[]{:S(2)}) collective-permute-start(f32[32,16,128]{2,1,0:T(8,128)S(1)} %add.300), channel_id=1, source_target_pairs={{0,32},{32,64},{64,96},{96,128},{128,160},{160,192},{192,224},{224... | collective-permute-start | bytes 786440 | tf_op jit(solution)/shard_map/while/body/eval_jaxpr/ppermute | solution.py:40
  523.4 6.0 copy-start.1
  523.4 8.6 %collective-permute-start = (bf16[32,16,128]{2,1,0:T(8,128)(2,1)S(1)}, bf16[32,16,128]{2,1,0:T(8,128)(2,1)S(1)}, u32[]{:S(2)}, u32[]{:S(2)}) collective-permute-start(bf16[32,16,128]{2,1,0:T(8,128)(2,1)S(1)} %copy.38), channel_id=1, source_target_pairs={{0,32},{32,64},{64,96},{96,128},{128,160},{160,192},{192,224},{224... | collective-permute-start | bytes 393224 | tf_op jit(solution)/shard_map/while/body/eval_jaxpr/ppermute | solution.py:40
  529.6 9.8 %collective-permute-start.1 = (f32[32,16,128]{2,1,0:T(8,128)S(1)}, f32[32,16,128]{2,1,0:T(8,128)S(1)}, u32[]{:S(2)}, u32[]{:S(2)}) collective-permute-start(f32[32,16,128]{2,1,0:T(8,128)S(1)} %add.300), channel_id=1, source_target_pairs={{0,32},{32,64},{64,96},{96,128},{128,160},{160,192},{192,224},{224... | collective-permute-start | bytes 786440 | tf_op jit(solution)/shard_map/while/body/eval_jaxpr/ppermute | solution.py:40
  539.4 6.0 copy-start.1
  539.4 8.6 %collective-permute-start = (bf16[32,16,128]{2,1,0:T(8,128)(2,1)S(1)}, bf16[32,16,128]{2,1,0:T(8,128)(2,1)S(1)}, u32[]{:S(2)}, u32[]{:S(2)}) collective-permute-start(bf16[32,16,128]{2,1,0:T(8,128)(2,1)S(1)} %copy.38), channel_id=1, source_target_pairs={{0,32},{32,64},{64,96},{96,128},{128,160},{160,192},{192,224},{224... | collective-permute-start | bytes 393224 | tf_op jit(solution)/shard_map/while/body/eval_jaxpr/ppermute | solution.py:40
  545.6 9.8 %collective-permute-start.1 = (f32[32,16,128]{2,1,0:T(8,128)S(1)}, f32[32,16,128]{2,1,0:T(8,128)S(1)}, u32[]{:S(2)}, u32[]{:S(2)}) collective-permute-start(f32[32,16,128]{2,1,0:T(8,128)S(1)} %add.300), channel_id=1, source_target_pairs={{0,32},{32,64},{64,96},{96,128},{128,160},{160,192},{192,224},{224... | collective-permute-start | bytes 786440 | tf_op jit(solution)/shard_map/while/body/eval_jaxpr/ppermute | solution.py:40
  555.4 6.0 copy-start.1
  555.4 8.6 %collective-permute-start = (bf16[32,16,128]{2,1,0:T(8,128)(2,1)S(1)}, bf16[32,16,128]{2,1,0:T(8,128)(2,1)S(1)}, u32[]{:S(2)}, u32[]{:S(2)}) collective-permute-start(bf16[32,16,128]{2,1,0:T(8,128)(2,1)S(1)} %copy.38), channel_id=1, source_target_pairs={{0,32},{32,64},{64,96},{96,128},{128,160},{160,192},{192,224},{224... | collective-permute-start | bytes 393224 | tf_op jit(solution)/shard_map/while/body/eval_jaxpr/ppermute | solution.py:40
  561.7 9.8 %collective-permute-start.1 = (f32[32,16,128]{2,1,0:T(8,128)S(1)}, f32[32,16,128]{2,1,0:T(8,128)S(1)}, u32[]{:S(2)}, u32[]{:S(2)}) collective-permute-start(f32[32,16,128]{2,1,0:T(8,128)S(1)} %add.300), channel_id=1, source_target_pairs={{0,32},{32,64},{64,96},{96,128},{128,160},{160,192},{192,224},{224... | collective-permute-start | bytes 786440 | tf_op jit(solution)/shard_map/while/body/eval_jaxpr/ppermute | solution.py:40
  571.5 6.0 copy-start.1
  571.5 8.6 %collective-permute-start = (bf16[32,16,128]{2,1,0:T(8,128)(2,1)S(1)}, bf16[32,16,128]{2,1,0:T(8,128)(2,1)S(1)}, u32[]{:S(2)}, u32[]{:S(2)}) collective-permute-start(bf16[32,16,128]{2,1,0:T(8,128)(2,1)S(1)} %copy.38), channel_id=1, source_target_pairs={{0,32},{32,64},{64,96},{96,128},{128,160},{160,192},{192,224},{224... | collective-permute-start | bytes 393224 | tf_op jit(solution)/shard_map/while/body/eval_jaxpr/ppermute | solution.py:40
  577.7 9.8 %collective-permute-start.1 = (f32[32,16,128]{2,1,0:T(8,128)S(1)}, f32[32,16,128]{2,1,0:T(8,128)S(1)}, u32[]{:S(2)}, u32[]{:S(2)}) collective-permute-start(f32[32,16,128]{2,1,0:T(8,128)S(1)} %add.300), channel_id=1, source_target_pairs={{0,32},{32,64},{64,96},{96,128},{128,160},{160,192},{192,224},{224... | collective-permute-start | bytes 786440 | tf_op jit(solution)/shard_map/while/body/eval_jaxpr/ppermute | solution.py:40
  587.5 6.0 copy-start.1
  587.5 8.6 %collective-permute-start = (bf16[32,16,128]{2,1,0:T(8,128)(2,1)S(1)}, bf16[32,16,128]{2,1,0:T(8,128)(2,1)S(1)}, u32[]{:S(2)}, u32[]{:S(2)}) collective-permute-start(bf16[32,16,128]{2,1,0:T(8,128)(2,1)S(1)} %copy.38), channel_id=1, source_target_pairs={{0,32},{32,64},{64,96},{96,128},{128,160},{160,192},{192,224},{224... | collective-permute-start | bytes 393224 | tf_op jit(solution)/shard_map/while/body/eval_jaxpr/ppermute | solution.py:40
  593.7 9.8 %collective-permute-start.1 = (f32[32,16,128]{2,1,0:T(8,128)S(1)}, f32[32,16,128]{2,1,0:T(8,128)S(1)}, u32[]{:S(2)}, u32[]{:S(2)}) collective-permute-start(f32[32,16,128]{2,1,0:T(8,128)S(1)} %add.300), channel_id=1, source_target_pairs={{0,32},{32,64},{64,96},{96,128},{128,160},{160,192},{192,224},{224... | collective-permute-start | bytes 786440 | tf_op jit(solution)/shard_map/while/body/eval_jaxpr/ppermute | solution.py:40
  603.5 6.0 copy-start.1
  603.5 8.6 %collective-permute-start = (bf16[32,16,128]{2,1,0:T(8,128)(2,1)S(1)}, bf16[32,16,128]{2,1,0:T(8,128)(2,1)S(1)}, u32[]{:S(2)}, u32[]{:S(2)}) collective-permute-start(bf16[32,16,128]{2,1,0:T(8,128)(2,1)S(1)} %copy.38), channel_id=1, source_target_pairs={{0,32},{32,64},{64,96},{96,128},{128,160},{160,192},{192,224},{224... | collective-permute-start | bytes 393224 | tf_op jit(solution)/shard_map/while/body/eval_jaxpr/ppermute | solution.py:40
  609.7 9.8 %collective-permute-start.1 = (f32[32,16,128]{2,1,0:T(8,128)S(1)}, f32[32,16,128]{2,1,0:T(8,128)S(1)}, u32[]{:S(2)}, u32[]{:S(2)}) collective-permute-start(f32[32,16,128]{2,1,0:T(8,128)S(1)} %add.300), channel_id=1, source_target_pairs={{0,32},{32,64},{64,96},{96,128},{128,160},{160,192},{192,224},{224... | collective-permute-start | bytes 786440 | tf_op jit(solution)/shard_map/while/body/eval_jaxpr/ppermute | solution.py:40
  623.4 9.9 %collective-permute-start.2 = (f32[32,16,128]{2,1,0:T(8,128)S(1)}, f32[32,16,128]{2,1,0:T(8,128)}, u32[]{:S(2)}, u32[]{:S(2)}) collective-permute-start(f32[32,16,128]{2,1,0:T(8,128)S(1)} %add.247), channel_id=1, source_target_pairs={{0,32},{32,64},{64,96},{96,128},{128,160},{160,192},{192,224},{224... | collective-permute-start | bytes 786440 | tf_op jit(solution)/shard_map/ppermute | solution.py:40
  633.3 25.9 %all-to-all-start = ((f32[32,1,16,128]{3,2,1,0:T(8,128)}), f32[32,1,16,128]{3,2,1,0:T(8,128)S(1)}, u32[]{:S(2)}, u32[]{:S(2)}) async-start(f32[32,1,16,128]{3,2,1,0:T(8,128)} %bitcast.32), calls=%async_computation | async-start | bytes 524288 | tf_op jit(solution)/shard_map/all_to_all | solution.py:50
  641.4 18.5 %copy-start.2 = (f32[2,128,128]{2,1,0:T(8,128)}, f32[2,128,128]{2,1,0:T(8,128)S(1)}, u32[]{:S(2)}) copy-start(f32[2,128,128]{2,1,0:T(8,128)S(1)} %fusion.42) | copy-start | bytes 393220
Sparse Core Ops, SparseCore 0:
  94.6 31.2 all-gather.4
where the time goes:
time: 676 us; the launch traced here: 668 us
  blocking collectives  292 us (43%)
  waiting for transfers between devices  135 us (20%)
  matrix products  88 us (13%)
  starting transfers between devices  69.9 us (10%)
  other arithmetic  33.9 us (5%)
  local copies, waits for them, and re-layouts  29.3 us (4%)
  between operations  18 us (3%)
    ppermute x31, waiting for transfers between devices, from_behind(): return lax.ppermute(value, axis, pairs)  117 us
    all_gather x1, blocking collectives, on_device(): lax.all_gather(queries, GROUP, axis=0, tiled=True)  87.3 us
    all_gather x1, blocking collectives, side_by_side(): lax.all_gather(both, axis, axis=dim, tiled=True)  70.5 us
    ppermute x31, starting transfers between devices, from_behind(): return lax.ppermute(value, axis, pairs)  63.5 us
    dot_general x64, matrix products, masked_logits(): lax.dot_general(row_block, lone_document, (((1,), (1,)), ((), ())), prefe...  62.4 us
    pmax x5, blocking collectives, over_axes(): return functools.reduce(lax.pmax, axes, x)  54.4 us
    psum x5, blocking collectives, one_axis_at_a_time(): x = lax.psum(x, axis)  51.7 us
    broadcast_in_dim x32, other arithmetic, masked_logits(): jnp.where(live_image_embeddings[None, :] > 0, similarity_matrix / relaxat...  24.4 us
  transfers between devices with their start and end apart: 33, of which 17 were waited for; matrix products, arithmetic and copies ran while one was open for 11% of the time, Pallas kernels for 0%

commit v1 on v0

--- a/solution.py
+++ b/solution.py
@@ -72,7 +72,9 @@
     total_queries = bundle_size * blocks
     natural_logarithm_lengths = jnp.log(jnp.sum(page_mask.astype(jnp.float32), axis=1))
     bundle_vectors, bundle_masks, bundle_targets = (
-        lax.all_gather(queries, GROUP, axis=0, tiled=True),
+        jnp.concatenate(
+            lax.all_to_all(jnp.stack([queries] * lax.axis_size(GROUP)), GROUP, 0, 0), axis=0
+        ),
         *side_by_side((query_mask, positive), GROUP, 0, 1),
     )
 

time: 676 us -> 533 us (0.79)
  matrix products: 88 us -> 26.7 us
  blocking collectives: 292 us -> 241 us
  other arithmetic: 33.9 us -> 10.5 us
    all_gather x1 -> x0, blocking collectives: 87.3 us -> none  [on_device(): lax.all_gather(queries, GROUP, axis=0, tiled=True)]
    dot_general x64, matrix products: 62.4 us -> 14 us  [masked_logits(): lax.dot_general(row_block, lone_document, (((1,), (1,)), ((), ())), prefe...]
    all_to_all x0 -> x1, blocking collectives: none -> 35.3 us  [on_device(): lax.all_to_all(jnp.stack([queries] * lax.axis_size(GROUP)), GROUP, 0, 0)]
    broadcast_in_dim x32, other arithmetic: 24.4 us -> 1 us  [masked_logits(): jnp.where(live_image_embeddings[None, :] > 0, similarity_matrix / relaxat...]
    dot_general x32, matrix products: 18.2 us -> 5.32 us  [gradient_terms(): jnp.dot(factor, page_vectors[number], preferred_element_type=jnp.float32)]
  transfers between devices with their start and end apart: 33 -> 33, of which waited for: 17 -> 32; matrix products, arithmetic and copies ran while one was open for 11% -> 5% of each run, Pallas kernels for 0% -> 0%
where the time goes in v1:
time: 533 us; the launch traced here: 531 us
  blocking collectives  241 us (45%)
  waiting for transfers between devices  135 us (25%)
  starting transfers between devices  68 us (13%)
  local copies, waits for them, and re-layouts  30 us (6%)
  matrix products  26.7 us (5%)
  between operations  18 us (3%)
  other arithmetic  10.5 us (2%)
    ppermute x31, waiting for transfers between devices, from_behind(): return lax.ppermute(value, axis, pairs)  117 us
    all_gather x1, blocking collectives, side_by_side(): lax.all_gather(both, axis, axis=dim, tiled=True)  71.2 us
    ppermute x31, starting transfers between devices, from_behind(): return lax.ppermute(value, axis, pairs)  61.6 us
    pmax x5, blocking collectives, over_axes(): return functools.reduce(lax.pmax, axes, x)  53.6 us
    psum x5, blocking collectives, one_axis_at_a_time(): x = lax.psum(x, axis)  52.5 us
    all_to_all x1, blocking collectives, on_device(): lax.all_to_all(jnp.stack([queries] * lax.axis_size(GROUP)), GROUP, 0, 0)  35.3 us
    all_gather x1, blocking collectives, on_device(): lax.all_gather(bundle_masks, BLK, axis=0, tiled=True)  20.1 us
    all_to_all x1, waiting for transfers between devices, sum_at_owner(): pieces = lax.all_to_all(cut_along(x, dim, size), axis, 0, 0, tiled=True)  17.8 us
  transfers between devices with their start and end apart: 33, of which 32 were waited for; matrix products, arithmetic and copies ran while one was open for 5% of the time, Pallas kernels for 0%

profile of v1, /device:TPU:2, one launch (start us, length us, event | category | flops | bytes accessed | tf_op | source)
XLA Modules:
  0.0 530.9 jit_solution(1759099171696694886)
XLA Ops:
  7.9 35.3 %all_to_all.10 = bf16[32,1,16,128]{3,2,1,0:T(8,128)(2,1)} all-to-all(bf16[32,1,16,128]{3,2,1,0:T(8,128)(2,1)S(1)} %stack.10), channel_id=1, replica_groups=mesh['blk_0'=2,'blk_1'=4,'blk_2'=2,'group_0'=2,'group_1'=16] {'group_0',..., dimensions={0} | all-to-all | bytes 262144 | tf_op jit(solution)/shard_map/all_to_all | solution.py:76
  44.7 71.2 %all-gather.2 = s32[32,1,17]{2,1,0:T(1,128)S(1)} all-gather(s32[1,1,17]{2,1,0:T(1,128)S(1)} %add_bitcast_fusion), channel_id=1, replica_groups=mesh['blk_0'=2,'blk_1'=4,'blk_2'=2,'group_0'=2,'group_1'=16] {'group_0',..., dimensions={0}, use_global_device_ids=true | all-gather | bytes 2244 | tf_op jit(solution)/shard_map/all_gather | solution.py:19
  116.0 20.1 %all-gather.3 = s32[16,32,16]{1,2,0:T(8,128)S(1)} all-gather(s32[1,32,16]{1,2,0:T(8,128)S(1)} %copy.11), channel_id=1, replica_groups=mesh['blk_0'=2,'blk_1'=4,'blk_2'=2,'group_0'=2,'group_1'=16] {'blk_0','b..., dimensions={0}, use_global_device_ids=true | all-gather | bytes 34816 | tf_op jit(solution)/shard_map/all_gather | solution.py:127
  139.6 8.0 %all-reduce = s32[512]{0:T(512)S(1)} all-reduce(s32[512]{0:T(512)S(1)} %dynamic-update-slice.26), channel_id=3, replica_groups=mesh['blk_0'=2,'blk_1'=4,'blk_2'=2,'group_0'=2,'group_1'=16] {'blk_0','b..., use_global_device_ids=true, to_apply=%add | all-reduce | flops 512 | bytes 4096
  148.5 36.2 %while.38 = (s32[]{:T(128)}, f32[512,2]{0,1:T(2,128)S(1)}, f32[512,16,2]{1,0,2:T(8,128)S(1)}, s32[2,128]{1,0:T(2,128)S(1)}, bf16[512,16,128]{2,1,0:T(8,128)(2,1)...) while((s32[]{:T(128)}, f32[512,2]{0,1:T(2,128)S(1)}, ...), condition=%wide.region_7.8_spmd, body=%wide.region_1.7_spmd.sunk | while | flops 34213060 | bytes 1821107 | solution.py:110
  184.7 4.9 pmax.35
  189.6 11.6 %pmax.36 = f32[512]{0:T(512)S(1)} all-reduce(f32[512]{0:T(512)S(1)} %pmax.35), channel_id=1, replica_groups=mesh['blk_0'=2,'blk_1'=4,'blk_2'=2,'group_0'=2,'group_1'=16] {'blk_1'}, use_global_device_ids=true, to_apply=%region_10.11 | all-reduce | flops 512 | bytes 4096 | tf_op jit(solution)/shard_map/pmax | solution.py:28
  201.2 2.5 pmax.37
  203.7 6.4 %pmax.38 = f32[512]{0:T(512)S(1)} all-reduce(f32[512]{0:T(512)S(1)} %pmax.37), channel_id=1, replica_groups=mesh['blk_0'=2,'blk_1'=4,'blk_2'=2,'group_0'=2,'group_1'=16] {'group_0'}, use_global_device_ids=true, to_apply=%region_12.13 | all-reduce | flops 512 | bytes 4096 | tf_op jit(solution)/shard_map/pmax | solution.py:28
  210.1 28.2 %pmax.39 = f32[512]{0:T(512)S(1)} all-reduce(f32[512]{0:T(512)S(1)} %pmax.38), channel_id=1, replica_groups=mesh['blk_0'=2,'blk_1'=4,'blk_2'=2,'group_0'=2,'group_1'=16] {'group_1'}, use_global_device_ids=true, to_apply=%region_13.14 | all-reduce | flops 512 | bytes 4096 | tf_op jit(solution)/shard_map/pmax | solution.py:28
  239.0 5.5 %all-reduce.5 = (f32[512]{0:T(512)S(1)}, f32[]{:T(128)}) all-reduce(f32[512]{0:T(512)S(1)} %get-tuple-element.459, f32[]{:T(128)} %get-tuple-element.458), channel_id=1, replica_groups=mesh['blk_0'=2,'blk_1'=4,'blk_2'=2,'group_0'=2,'group_1'=16] {'blk_0'}, use_global_device_ids=true, to_apply=%region_15.16 | all-reduce | flops 513 | bytes 4104 | tf_op jit(solution)/shard_map/psum | solution.py:33
  244.5 8.3 %all-reduce.2 = (f32[512]{0:T(512)S(1)}, f32[]{:T(128)}) all-reduce(f32[512]{0:T(512)S(1)} %get-tuple-element.502, f32[]{:T(128)} %get-tuple-element.503), channel_id=1, replica_groups=mesh['blk_0'=2,'blk_1'=4,'blk_2'=2,'group_0'=2,'group_1'=16] {'blk_1'}, use_global_device_ids=true, to_apply=%region_16.17 | all-reduce | flops 513 | bytes 4104 | tf_op jit(solution)/shard_map/psum | solution.py:33
  252.9 3.1 all-reduce.4
  256.0 7.0 %all-reduce.3 = (f32[512]{0:T(512)S(1)}, f32[]{:T(128)}) all-reduce(f32[512]{0:T(512)S(1)} %get-tuple-element.500, f32[]{:T(128)} %get-tuple-element.501), channel_id=1, replica_groups=mesh['blk_0'=2,'blk_1'=4,'blk_2'=2,'group_0'=2,'group_1'=16] {'group_0'}, use_global_device_ids=true, to_apply=%region_18.19 | all-reduce | flops 513 | bytes 4104 | tf_op jit(solution)/shard_map/psum | solution.py:33
  263.0 28.4 %all-reduce.1 = (f32[512]{0:T(512)S(1)}, f32[]{:T(128)}) all-reduce(f32[512]{0:T(512)S(1)} %get-tuple-element.498, f32[]{:T(128)} %get-tuple-element.499), channel_id=1, replica_groups=mesh['blk_0'=2,'blk_1'=4,'blk_2'=2,'group_0'=2,'group_1'=16] {'group_1'}, use_global_device_ids=true, to_apply=%region_19.20 | all-reduce | flops 513 | bytes 4104 | tf_op jit(solution)/shard_map/psum | solution.py:33
  292.7 192.9 %while.39 = (s32[]{:T(128)}, bf16[32,16,128]{2,1,0:T(8,128)(2,1)S(1)}, f32[32,16,128]{2,1,0:T(8,128)S(1)}, f32[2,128,128]{2,1,0:T(8,128)S(1)}, s32[]{:T(128)}, /...) while((s32[]{:T(128)}, ...), condition=%wide.region_21.22_spmd, body=%wide.region_20.21_spmd.sunk | while | flops 101482768 | bytes 5171848 | solution.py:193
  292.7 1.9 collective-permute-start
  295.8 4.0 collective-permute-start.1
  301.1 4.5 collective-permute-done.1
  305.6 1.9 collective-permute-start
  308.6 1.9 collective-permute-start.1
  311.0 2.9 collective-permute-done
  314.0 4.5 collective-permute-done.1
  318.4 1.9 collective-permute-start
  321.5 1.9 collective-permute-start.1
  323.9 2.9 collective-permute-done
  326.8 4.5 collective-permute-done.1
  331.3 1.9 collective-permute-start
  334.3 1.9 collective-permute-start.1
  336.8 2.9 collective-permute-done
  339.7 4.5 collective-permute-done.1
  344.2 1.9 collective-permute-start
  349.6 2.9 collective-permute-done
  352.6 4.4 collective-permute-done.1
  357.0 1.9 collective-permute-start
  362.5 2.9 collective-permute-done
  365.4 4.4 collective-permute-done.1
  372.9 1.9 collective-permute-start.1
  375.3 2.9 collective-permute-done
  378.3 4.4 collective-permute-done.1
  388.2 2.9 collective-permute-done
  391.1 4.4 collective-permute-done.1
  401.0 2.9 collective-permute-done
  404.0 4.4 collective-permute-done.1
  411.5 1.9 collective-permute-start.1
  413.9 2.9 collective-permute-done
  416.9 4.4 collective-permute-done.1
  421.3 1.9 collective-permute-start
  426.8 2.9 collective-permute-done
  429.7 4.4 collective-permute-done.1
  439.6 2.9 collective-permute-done
  442.6 4.4 collective-permute-done.1
  452.5 2.9 collective-permute-done
  455.4 4.4 collective-permute-done.1
  459.9 1.9 collective-permute-start
  465.3 2.9 collective-permute-done
  468.3 4.4 collective-permute-done.1
  475.8 1.9 collective-permute-start.1
  478.2 2.9 collective-permute-done
  481.2 4.4 collective-permute-done.1
  486.5 1.9 collective-permute-start.2
  488.4 8.0 %collective-permute-done.2 = f32[32,16,128]{2,1,0:T(8,128)} collective-permute-done((f32[32,16,128]{2,1,0:T(8,128)S(1)}, f32[32,16,128]{2,1,0:T(8,128)}, u32[]{:S(2)}, u32[]{:S(2)}) %collective-permute-start.2) | collective-permute-done | bytes 262176 | tf_op jit(solution)/shard_map/ppermute | solution.py:40
  496.4 6.3 %all-to-all-start.1 = ((f32[32,1,16,128]{3,2,1,0:T(8,128)}), f32[32,1,16,128]{3,2,1,0:T(8,128)S(1)}, u32[]{:S(2)}, u32[]{:S(2)}) async-start(f32[32,1,16,128]{3,2,1,0:T(8,128)} %bitcast.35), calls=%async_computation.1 | async-start | bytes 524288 | tf_op jit(solution)/shard_map/all_to_all | solution.py:50
  504.5 17.8 %all-to-all-done.1 = f32[32,1,16,128]{3,2,1,0:T(8,128)S(1)} async-done(((f32[32,1,16,128]{3,2,1,0:T(8,128)}), f32[32,1,16,128]{3,2,1,0:T(8,128)S(1)}, u32[]{:S(2)}, u32[]{:S(2)}) %all-to-all-start.1) | async-done | bytes 262176 | tf_op jit(solution)/shard_map/all_to_all | solution.py:50
  (548 shorter events, 96.8 us)
Async XLA Ops:
  7.2 141.3 %copy-start.3 = (s32[2,128]{1,0:T(2,128)S(1)}, s32[2,128]{1,0:T(2,128)}, u32[]{:S(2)}) copy-start(s32[2,128]{1,0:T(2,128)} %param.21) | copy-start | bytes 3076
  7.2 141.3 %copy-start.1 = (bf16[2,128,128]{2,1,0:T(8,128)(2,1)S(1)}, bf16[2,128,128]{2,1,0:T(8,128)(2,1)}, u32[]{:S(2)}) copy-start(bf16[2,128,128]{2,1,0:T(8,128)(2,1)} %param.20) | copy-start | bytes 196612
  7.2 141.2 %all-gather.6.cloned.1.call-start = ((), (), s32[]{:S(2)}) async-start(), calls=%async_computation.2 | async-start | bytes 2228224 | tf_op jit(solution)/shard_map/all_gather | solution.py:126
  148.5 144.2 %copy-start = (bf16[32,1,16,128]{3,2,1,0:T(8,128)(2,1)S(1)}, bf16[32,1,16,128]{3,2,1,0:T(8,128)(2,1)}, u32[]{:S(2)}) copy-start(bf16[32,1,16,128]{3,2,1,0:T(8,128)(2,1)} %all_to_all.10) | copy-start | bytes 393220
  292.7 8.4 %collective-permute-start = (bf16[32,16,128]{2,1,0:T(8,128)(2,1)S(1)}, bf16[32,16,128]{2,1,0:T(8,128)(2,1)S(1)}, u32[]{:S(2)}, u32[]{:S(2)}) collective-permute-start(bf16[32,16,128]{2,1,0:T(8,128)(2,1)S(1)} %copy.38), channel_id=1, source_target_pairs={{0,32},{32,64},{64,96},{96,128},{128,160},{160,192},{192,224},{224... | collective-permute-start | bytes 393224 | tf_op jit(solution)/shard_map/while/body/eval_jaxpr/ppermute | solution.py:40
  295.8 9.8 %collective-permute-start.1 = (f32[32,16,128]{2,1,0:T(8,128)S(1)}, f32[32,16,128]{2,1,0:T(8,128)S(1)}, u32[]{:S(2)}, u32[]{:S(2)}) collective-permute-start(f32[32,16,128]{2,1,0:T(8,128)S(1)} %add.300), channel_id=1, source_target_pairs={{0,32},{32,64},{64,96},{96,128},{128,160},{160,192},{192,224},{224... | collective-permute-start | bytes 786440 | tf_op jit(solution)/shard_map/while/body/eval_jaxpr/ppermute | solution.py:40
  305.6 8.4 %collective-permute-start = (bf16[32,16,128]{2,1,0:T(8,128)(2,1)S(1)}, bf16[32,16,128]{2,1,0:T(8,128)(2,1)S(1)}, u32[]{:S(2)}, u32[]{:S(2)}) collective-permute-start(bf16[32,16,128]{2,1,0:T(8,128)(2,1)S(1)} %copy.38), channel_id=1, source_target_pairs={{0,32},{32,64},{64,96},{96,128},{128,160},{160,192},{192,224},{224... | collective-permute-start | bytes 393224 | tf_op jit(solution)/shard_map/while/body/eval_jaxpr/ppermute | solution.py:40
  308.6 9.8 %collective-permute-start.1 = (f32[32,16,128]{2,1,0:T(8,128)S(1)}, f32[32,16,128]{2,1,0:T(8,128)S(1)}, u32[]{:S(2)}, u32[]{:S(2)}) collective-permute-start(f32[32,16,128]{2,1,0:T(8,128)S(1)} %add.300), channel_id=1, source_target_pairs={{0,32},{32,64},{64,96},{96,128},{128,160},{160,192},{192,224},{224... | collective-permute-start | bytes 786440 | tf_op jit(solution)/shard_map/while/body/eval_jaxpr/ppermute | solution.py:40
  318.4 8.4 %collective-permute-start = (bf16[32,16,128]{2,1,0:T(8,128)(2,1)S(1)}, bf16[32,16,128]{2,1,0:T(8,128)(2,1)S(1)}, u32[]{:S(2)}, u32[]{:S(2)}) collective-permute-start(bf16[32,16,128]{2,1,0:T(8,128)(2,1)S(1)} %copy.38), channel_id=1, source_target_pairs={{0,32},{32,64},{64,96},{96,128},{128,160},{160,192},{192,224},{224... | collective-permute-start | bytes 393224 | tf_op jit(solution)/shard_map/while/body/eval_jaxpr/ppermute | solution.py:40
  321.5 9.8 %collective-permute-start.1 = (f32[32,16,128]{2,1,0:T(8,128)S(1)}, f32[32,16,128]{2,1,0:T(8,128)S(1)}, u32[]{:S(2)}, u32[]{:S(2)}) collective-permute-start(f32[32,16,128]{2,1,0:T(8,128)S(1)} %add.300), channel_id=1, source_target_pairs={{0,32},{32,64},{64,96},{96,128},{128,160},{160,192},{192,224},{224... | collective-permute-start | bytes 786440 | tf_op jit(solution)/shard_map/while/body/eval_jaxpr/ppermute | solution.py:40
  331.3 8.4 %collective-permute-start = (bf16[32,16,128]{2,1,0:T(8,128)(2,1)S(1)}, bf16[32,16,128]{2,1,0:T(8,128)(2,1)S(1)}, u32[]{:S(2)}, u32[]{:S(2)}) collective-permute-start(bf16[32,16,128]{2,1,0:T(8,128)(2,1)S(1)} %copy.38), channel_id=1, source_target_pairs={{0,32},{32,64},{64,96},{96,128},{128,160},{160,192},{192,224},{224... | collective-permute-start | bytes 393224 | tf_op jit(solution)/shard_map/while/body/eval_jaxpr/ppermute | solution.py:40
  334.3 9.8 %collective-permute-start.1 = (f32[32,16,128]{2,1,0:T(8,128)S(1)}, f32[32,16,128]{2,1,0:T(8,128)S(1)}, u32[]{:S(2)}, u32[]{:S(2)}) collective-permute-start(f32[32,16,128]{2,1,0:T(8,128)S(1)} %add.300), channel_id=1, source_target_pairs={{0,32},{32,64},{64,96},{96,128},{128,160},{160,192},{192,224},{224... | collective-permute-start | bytes 786440 | tf_op jit(solution)/shard_map/while/body/eval_jaxpr/ppermute | solution.py:40
  344.2 8.4 %collective-permute-start = (bf16[32,16,128]{2,1,0:T(8,128)(2,1)S(1)}, bf16[32,16,128]{2,1,0:T(8,128)(2,1)S(1)}, u32[]{:S(2)}, u32[]{:S(2)}) collective-permute-start(bf16[32,16,128]{2,1,0:T(8,128)(2,1)S(1)} %copy.38), channel_id=1, source_target_pairs={{0,32},{32,64},{64,96},{96,128},{128,160},{160,192},{192,224},{224... | collective-permute-start | bytes 393224 | tf_op jit(solution)/shard_map/while/body/eval_jaxpr/ppermute | solution.py:40
  347.2 9.8 %collective-permute-start.1 = (f32[32,16,128]{2,1,0:T(8,128)S(1)}, f32[32,16,128]{2,1,0:T(8,128)S(1)}, u32[]{:S(2)}, u32[]{:S(2)}) collective-permute-start(f32[32,16,128]{2,1,0:T(8,128)S(1)} %add.300), channel_id=1, source_target_pairs={{0,32},{32,64},{64,96},{96,128},{128,160},{160,192},{192,224},{224... | collective-permute-start | bytes 786440 | tf_op jit(solution)/shard_map/while/body/eval_jaxpr/ppermute | solution.py:40
  357.0 8.4 %collective-permute-start = (bf16[32,16,128]{2,1,0:T(8,128)(2,1)S(1)}, bf16[32,16,128]{2,1,0:T(8,128)(2,1)S(1)}, u32[]{:S(2)}, u32[]{:S(2)}) collective-permute-start(bf16[32,16,128]{2,1,0:T(8,128)(2,1)S(1)} %copy.38), channel_id=1, source_target_pairs={{0,32},{32,64},{64,96},{96,128},{128,160},{160,192},{192,224},{224... | collective-permute-start | bytes 393224 | tf_op jit(solution)/shard_map/while/body/eval_jaxpr/ppermute | solution.py:40
  360.1 9.8 %collective-permute-start.1 = (f32[32,16,128]{2,1,0:T(8,128)S(1)}, f32[32,16,128]{2,1,0:T(8,128)S(1)}, u32[]{:S(2)}, u32[]{:S(2)}) collective-permute-start(f32[32,16,128]{2,1,0:T(8,128)S(1)} %add.300), channel_id=1, source_target_pairs={{0,32},{32,64},{64,96},{96,128},{128,160},{160,192},{192,224},{224... | collective-permute-start | bytes 786440 | tf_op jit(solution)/shard_map/while/body/eval_jaxpr/ppermute | solution.py:40
  369.9 8.4 %collective-permute-start = (bf16[32,16,128]{2,1,0:T(8,128)(2,1)S(1)}, bf16[32,16,128]{2,1,0:T(8,128)(2,1)S(1)}, u32[]{:S(2)}, u32[]{:S(2)}) collective-permute-start(bf16[32,16,128]{2,1,0:T(8,128)(2,1)S(1)} %copy.38), channel_id=1, source_target_pairs={{0,32},{32,64},{64,96},{96,128},{128,160},{160,192},{192,224},{224... | collective-permute-start | bytes 393224 | tf_op jit(solution)/shard_map/while/body/eval_jaxpr/ppermute | solution.py:40
  372.9 9.8 %collective-permute-start.1 = (f32[32,16,128]{2,1,0:T(8,128)S(1)}, f32[32,16,128]{2,1,0:T(8,128)S(1)}, u32[]{:S(2)}, u32[]{:S(2)}) collective-permute-start(f32[32,16,128]{2,1,0:T(8,128)S(1)} %add.300), channel_id=1, source_target_pairs={{0,32},{32,64},{64,96},{96,128},{128,160},{160,192},{192,224},{224... | collective-permute-start | bytes 786440 | tf_op jit(solution)/shard_map/while/body/eval_jaxpr/ppermute | solution.py:40
  382.7 8.4 %collective-permute-start = (bf16[32,16,128]{2,1,0:T(8,128)(2,1)S(1)}, bf16[32,16,128]{2,1,0:T(8,128)(2,1)S(1)}, u32[]{:S(2)}, u32[]{:S(2)}) collective-permute-start(bf16[32,16,128]{2,1,0:T(8,128)(2,1)S(1)} %copy.38), channel_id=1, source_target_pairs={{0,32},{32,64},{64,96},{96,128},{128,160},{160,192},{192,224},{224... | collective-permute-start | bytes 393224 | tf_op jit(solution)/shard_map/while/body/eval_jaxpr/ppermute | solution.py:40
  385.8 9.8 %collective-permute-start.1 = (f32[32,16,128]{2,1,0:T(8,128)S(1)}, f32[32,16,128]{2,1,0:T(8,128)S(1)}, u32[]{:S(2)}, u32[]{:S(2)}) collective-permute-start(f32[32,16,128]{2,1,0:T(8,128)S(1)} %add.300), channel_id=1, source_target_pairs={{0,32},{32,64},{64,96},{96,128},{128,160},{160,192},{192,224},{224... | collective-permute-start | bytes 786440 | tf_op jit(solution)/shard_map/while/body/eval_jaxpr/ppermute | solution.py:40
  395.6 8.4 %collective-permute-start = (bf16[32,16,128]{2,1,0:T(8,128)(2,1)S(1)}, bf16[32,16,128]{2,1,0:T(8,128)(2,1)S(1)}, u32[]{:S(2)}, u32[]{:S(2)}) collective-permute-start(bf16[32,16,128]{2,1,0:T(8,128)(2,1)S(1)} %copy.38), channel_id=1, source_target_pairs={{0,32},{32,64},{64,96},{96,128},{128,160},{160,192},{192,224},{224... | collective-permute-start | bytes 393224 | tf_op jit(solution)/shard_map/while/body/eval_jaxpr/ppermute | solution.py:40
  398.6 9.8 %collective-permute-start.1 = (f32[32,16,128]{2,1,0:T(8,128)S(1)}, f32[32,16,128]{2,1,0:T(8,128)S(1)}, u32[]{:S(2)}, u32[]{:S(2)}) collective-permute-start(f32[32,16,128]{2,1,0:T(8,128)S(1)} %add.300), channel_id=1, source_target_pairs={{0,32},{32,64},{64,96},{96,128},{128,160},{160,192},{192,224},{224... | collective-permute-start | bytes 786440 | tf_op jit(solution)/shard_map/while/body/eval_jaxpr/ppermute | solution.py:40
  408.5 8.4 %collective-permute-start = (bf16[32,16,128]{2,1,0:T(8,128)(2,1)S(1)}, bf16[32,16,128]{2,1,0:T(8,128)(2,1)S(1)}, u32[]{:S(2)}, u32[]{:S(2)}) collective-permute-start(bf16[32,16,128]{2,1,0:T(8,128)(2,1)S(1)} %copy.38), channel_id=1, source_target_pairs={{0,32},{32,64},{64,96},{96,128},{128,160},{160,192},{192,224},{224... | collective-permute-start | bytes 393224 | tf_op jit(solution)/shard_map/while/body/eval_jaxpr/ppermute | solution.py:40
  411.5 9.8 %collective-permute-start.1 = (f32[32,16,128]{2,1,0:T(8,128)S(1)}, f32[32,16,128]{2,1,0:T(8,128)S(1)}, u32[]{:S(2)}, u32[]{:S(2)}) collective-permute-start(f32[32,16,128]{2,1,0:T(8,128)S(1)} %add.300), channel_id=1, source_target_pairs={{0,32},{32,64},{64,96},{96,128},{128,160},{160,192},{192,224},{224... | collective-permute-start | bytes 786440 | tf_op jit(solution)/shard_map/while/body/eval_jaxpr/ppermute | solution.py:40
  421.3 8.4 %collective-permute-start = (bf16[32,16,128]{2,1,0:T(8,128)(2,1)S(1)}, bf16[32,16,128]{2,1,0:T(8,128)(2,1)S(1)}, u32[]{:S(2)}, u32[]{:S(2)}) collective-permute-start(bf16[32,16,128]{2,1,0:T(8,128)(2,1)S(1)} %copy.38), channel_id=1, source_target_pairs={{0,32},{32,64},{64,96},{96,128},{128,160},{160,192},{192,224},{224... | collective-permute-start | bytes 393224 | tf_op jit(solution)/shard_map/while/body/eval_jaxpr/ppermute | solution.py:40
  424.4 9.8 %collective-permute-start.1 = (f32[32,16,128]{2,1,0:T(8,128)S(1)}, f32[32,16,128]{2,1,0:T(8,128)S(1)}, u32[]{:S(2)}, u32[]{:S(2)}) collective-permute-start(f32[32,16,128]{2,1,0:T(8,128)S(1)} %add.300), channel_id=1, source_target_pairs={{0,32},{32,64},{64,96},{96,128},{128,160},{160,192},{192,224},{224... | collective-permute-start | bytes 786440 | tf_op jit(solution)/shard_map/while/body/eval_jaxpr/ppermute | solution.py:40
  434.2 8.4 %collective-permute-start = (bf16[32,16,128]{2,1,0:T(8,128)(2,1)S(1)}, bf16[32,16,128]{2,1,0:T(8,128)(2,1)S(1)}, u32[]{:S(2)}, u32[]{:S(2)}) collective-permute-start(bf16[32,16,128]{2,1,0:T(8,128)(2,1)S(1)} %copy.38), channel_id=1, source_target_pairs={{0,32},{32,64},{64,96},{96,128},{128,160},{160,192},{192,224},{224... | collective-permute-start | bytes 393224 | tf_op jit(solution)/shard_map/while/body/eval_jaxpr/ppermute | solution.py:40
  437.2 9.8 %collective-permute-start.1 = (f32[32,16,128]{2,1,0:T(8,128)S(1)}, f32[32,16,128]{2,1,0:T(8,128)S(1)}, u32[]{:S(2)}, u32[]{:S(2)}) collective-permute-start(f32[32,16,128]{2,1,0:T(8,128)S(1)} %add.300), channel_id=1, source_target_pairs={{0,32},{32,64},{64,96},{96,128},{128,160},{160,192},{192,224},{224... | collective-permute-start | bytes 786440 | tf_op jit(solution)/shard_map/while/body/eval_jaxpr/ppermute | solution.py:40
  447.0 8.4 %collective-permute-start = (bf16[32,16,128]{2,1,0:T(8,128)(2,1)S(1)}, bf16[32,16,128]{2,1,0:T(8,128)(2,1)S(1)}, u32[]{:S(2)}, u32[]{:S(2)}) collective-permute-start(bf16[32,16,128]{2,1,0:T(8,128)(2,1)S(1)} %copy.38), channel_id=1, source_target_pairs={{0,32},{32,64},{64,96},{96,128},{128,160},{160,192},{192,224},{224... | collective-permute-start | bytes 393224 | tf_op jit(solution)/shard_map/while/body/eval_jaxpr/ppermute | solution.py:40
  450.1 9.8 %collective-permute-start.1 = (f32[32,16,128]{2,1,0:T(8,128)S(1)}, f32[32,16,128]{2,1,0:T(8,128)S(1)}, u32[]{:S(2)}, u32[]{:S(2)}) collective-permute-start(f32[32,16,128]{2,1,0:T(8,128)S(1)} %add.300), channel_id=1, source_target_pairs={{0,32},{32,64},{64,96},{96,128},{128,160},{160,192},{192,224},{224... | collective-permute-start | bytes 786440 | tf_op jit(solution)/shard_map/while/body/eval_jaxpr/ppermute | solution.py:40
  459.9 8.4 %collective-permute-start = (bf16[32,16,128]{2,1,0:T(8,128)(2,1)S(1)}, bf16[32,16,128]{2,1,0:T(8,128)(2,1)S(1)}, u32[]{:S(2)}, u32[]{:S(2)}) collective-permute-start(bf16[32,16,128]{2,1,0:T(8,128)(2,1)S(1)} %copy.38), channel_id=1, source_target_pairs={{0,32},{32,64},{64,96},{96,128},{128,160},{160,192},{192,224},{224... | collective-permute-start | bytes 393224 | tf_op jit(solution)/shard_map/while/body/eval_jaxpr/ppermute | solution.py:40
  462.9 9.8 %collective-permute-start.1 = (f32[32,16,128]{2,1,0:T(8,128)S(1)}, f32[32,16,128]{2,1,0:T(8,128)S(1)}, u32[]{:S(2)}, u32[]{:S(2)}) collective-permute-start(f32[32,16,128]{2,1,0:T(8,128)S(1)} %add.300), channel_id=1, source_target_pairs={{0,32},{32,64},{64,96},{96,128},{128,160},{160,192},{192,224},{224... | collective-permute-start | bytes 786440 | tf_op jit(solution)/shard_map/while/body/eval_jaxpr/ppermute | solution.py:40
  472.8 8.4 %collective-permute-start = (bf16[32,16,128]{2,1,0:T(8,128)(2,1)S(1)}, bf16[32,16,128]{2,1,0:T(8,128)(2,1)S(1)}, u32[]{:S(2)}, u32[]{:S(2)}) collective-permute-start(bf16[32,16,128]{2,1,0:T(8,128)(2,1)S(1)} %copy.38), channel_id=1, source_target_pairs={{0,32},{32,64},{64,96},{96,128},{128,160},{160,192},{192,224},{224... | collective-permute-start | bytes 393224 | tf_op jit(solution)/shard_map/while/body/eval_jaxpr/ppermute | solution.py:40
  475.8 9.8 %collective-permute-start.1 = (f32[32,16,128]{2,1,0:T(8,128)S(1)}, f32[32,16,128]{2,1,0:T(8,128)S(1)}, u32[]{:S(2)}, u32[]{:S(2)}) collective-permute-start(f32[32,16,128]{2,1,0:T(8,128)S(1)} %add.300), channel_id=1, source_target_pairs={{0,32},{32,64},{64,96},{96,128},{128,160},{160,192},{192,224},{224... | collective-permute-start | bytes 786440 | tf_op jit(solution)/shard_map/while/body/eval_jaxpr/ppermute | solution.py:40
  486.5 9.9 %collective-permute-start.2 = (f32[32,16,128]{2,1,0:T(8,128)S(1)}, f32[32,16,128]{2,1,0:T(8,128)}, u32[]{:S(2)}, u32[]{:S(2)}) collective-permute-start(f32[32,16,128]{2,1,0:T(8,128)S(1)} %add.247), channel_id=1, source_target_pairs={{0,32},{32,64},{64,96},{96,128},{128,160},{160,192},{192,224},{224... | collective-permute-start | bytes 786440 | tf_op jit(solution)/shard_map/ppermute | solution.py:40
  496.4 25.9 %all-to-all-start.1 = ((f32[32,1,16,128]{3,2,1,0:T(8,128)}), f32[32,1,16,128]{3,2,1,0:T(8,128)S(1)}, u32[]{:S(2)}, u32[]{:S(2)}) async-start(f32[32,1,16,128]{3,2,1,0:T(8,128)} %bitcast.35), calls=%async_computation.1 | async-start | bytes 524288 | tf_op jit(solution)/shard_map/all_to_all | solution.py:50
  504.4 18.5 %copy-start.2 = (f32[2,128,128]{2,1,0:T(8,128)}, f32[2,128,128]{2,1,0:T(8,128)S(1)}, u32[]{:S(2)}) copy-start(f32[2,128,128]{2,1,0:T(8,128)S(1)} %fusion.42) | copy-start | bytes 393220
Sparse Core Ops, SparseCore 0:
  43.4 31.1 all-gather.5
